TPU v7x, 32 devices: a whole 2x2x4 slice. The times are simulated.
32 devices in a mesh: batch: 4 (over z), row: 4 (over x, core), col: 2 (over y).
Axes of the slice: x: 2, y: 2, z: 4, core: 2. Of those that a mesh axis runs over, the one named last changes fastest.
Arguments:
- flows: float32 [32768, 8192], P(('batch', 'row'), 'col'), parts along dimension 0, may hold values from 0 to 21, as said below
- tile_mask: int32 [256, 64], P(('batch', 'row'), 'col'), parts along dimension 0, may hold values from 0 to 1, as said below
- row_target: int32 [32768], P(('batch', 'row')), parts along dimension 0, may hold values from 1638400 to 8191999
- col_target: int32 [32768], P(('batch', 'col')), parts along dimension 0, may hold values from 1638400 to 8191999
Outputs:
- row_history: float32 [12, 8192], P('batch', 'row'), parts along dimension 0
- col_history: float32 [12, 8192], P('batch', 'col'), parts along dimension 0
There are 4 independent parts, one for each index of `batch`. A program takes and returns all parts, laid end to end along the dimension named above; each array names one. Nothing has to cross between parts.
Inputs may be any that keep to these rules, and one draw needn't show every extreme that they name: `tile_mask`: every diagonal tile is 1. `flows`: every entry is positive.
All inputs are finite; a program needn't handle non-finite values.
Results may differ from a plain program's by a relative error of at most 0.0001.
Values sent between devices are 32-bit elements; how exact they have to be, the bound alone decides.
A program may use at most 192 MiB of HBM per device.

v0:
```python
import jax
import jax.numpy as jnp
from jax import lax
from jax.sharding import PartitionSpec as P

ITERS = 3


def block_sweeps(active, row_goal, col_goal):
    row_count, col_count = active.shape
    row_hist = jnp.zeros((ITERS, row_count), jnp.float32)
    col_hist = jnp.zeros((ITERS, col_count), jnp.float32)
    col_scale = jnp.ones((col_count,), jnp.float32)

    def advance(sweep_index, carry):
        col_scale, row_hist, col_hist = carry
        row_part = jnp.sum(active * col_scale[None, :], axis=1)
        row_total = lax.psum(row_part, "col")
        row_scale = row_goal / row_total
        col_part = jnp.sum(active * row_scale[:, None], axis=0)
        col_total = lax.psum(col_part, "row")
        col_scale = col_goal / col_total
        row_hist = lax.dynamic_update_slice_in_dim(row_hist, row_scale[None, :], sweep_index, 0)
        col_hist = lax.dynamic_update_slice_in_dim(col_hist, col_scale[None, :], sweep_index, 0)
        return (col_scale, row_hist, col_hist)

    col_scale, row_hist, col_hist = lax.fori_loop(
        0, ITERS, advance, (col_scale, row_hist, col_hist)
    )
    return (row_hist, col_hist)


def shards(flows, tile_mask, row_target, col_target):
    row_count, col_count = flows.shape
    tile_side = row_count // tile_mask.shape[0]
    expand = tile_mask.astype(jnp.float32)[:, None, :, None]
    active = (
        flows.reshape(row_count // tile_side, tile_side, col_count // tile_side, tile_side) * expand
    ).reshape(row_count, col_count)
    row_goal = row_target.astype(jnp.float32) * 0.001
    col_goal = col_target.astype(jnp.float32) * 0.001
    row_hist, col_hist = block_sweeps(active, row_goal, col_goal)
    return (row_hist, col_hist)


def solution(mesh):
    return jax.shard_map(
        shards,
        mesh=mesh,
        in_specs=(
            P(("batch", "row"), "col"),
            P(("batch", "row"), "col"),
            P(("batch", "row")),
            P(("batch", "col")),
        ),
        out_specs=(P("batch", "row"), P("batch", "col")),
        check_vma=False,
    )
```

profile of v0, /device:TPU:0, one launch (start us, length us, event | category | flops | bytes accessed | tf_op | source)
XLA Modules:
  0.0 185.6 jit_solution(14115084264689669346)
XLA Ops:
  0.6 0.7 convert_element_type.9
  1.3 11.2 %mul.63 = f32[16,128,32,128]{3,2,1,0:T(8,128)} broadcast(f32[16,32]{1,0:T(8,128)S(1)} %convert_element_type.9), dimensions={0,2} | broadcast | bytes 33556480 | tf_op jit(solution)/shard_map/mul | solution.py:38
  12.6 42.4 %bitcast_multiply_fusion = f32[2048,4096]{1,0:T(8,128)} fusion(f32[2048,4096]{1,0:T(8,128)} %param.6, f32[256,8,32,128]{3,2,1,0:T(8,128)} %bitcast.10), kind=kLoop, calls=%fused_computation.3 | loop fusion | flops 8388608 | bytes 100663296 | tf_op jit(solution)/shard_map/mul | solution.py:38
  55.0 0.0 copy-done
  55.0 0.0 copy-done.1
  55.0 130.6 %while.18 = (s32[]{:T(128)}, f32[4096]{0:T(1024)S(1)}, f32[3,2048]{1,0:T(4,128)}, f32[3,4096]{1,0:T(4,128)}, f32[2048,4096]{1,0:T(8,128)}, /*index=5*/f32[2048]{0:T(1024)S(1)}, f32[4096]{0:T(1024)S(1)}, s32[]{:T(128)}, s32[]{:T(128)}) while((s32[]{:T(128)}, f32[4096]{0:T(1024)S(1)}, f32[3,2048]{1,0:T(4,128)}, f32[3,4096]{1,0:T(4,128)}, ...), condition=%wide.region_5.0_spmd.clone, body=%wide.region_0.0_spmd.clone.sunk | while | flops 33564672 | bytes 67362928 | solution.py:27
  55.1 12.3 %multiply_reduce_fusion.4 = f32[2048]{0:T(1024)S(1)} fusion(f32[2048,4096]{1,0:T(8,128)} %get-tuple-element.232, f32[4096]{0:T(1024)S(1)} %broadcast_select_fusion.2), kind=kLoop, calls=%fused_computation.1.clone.1 | loop fusion | flops 16775168 | bytes 33579008 | tf_op jit(solution)/shard_map/while/body/eval_jaxpr/reduce_sum | solution.py:17
  67.3 6.0 %psum.26 = f32[2048]{0:T(1024)S(1)} all-reduce(f32[2048]{0:T(1024)S(1)} %multiply_reduce_fusion.4), channel_id=1, replica_groups=mesh['batch'=4,'row'=4,'col'=2] {'col'}, use_global_device_ids=true, to_apply=%region_2.0 | all-reduce | flops 2048 | bytes 16384 | tf_op jit(solution)/shard_map/while/body/eval_jaxpr/psum | solution.py:18
  73.3 12.8 %multiply_reduce_fusion.5 = f32[4096]{0:T(1024)S(1)} fusion(f32[2048,4096]{1,0:T(8,128)} %get-tuple-element.232, f32[2048]{0:T(1024)S(1)} %div.18), kind=kLoop, calls=%fused_computation.clone.1 | loop fusion | flops 16773120 | bytes 33579008 | tf_op jit(solution)/shard_map/while/body/eval_jaxpr/reduce_sum | solution.py:20
  86.1 10.3 %psum.27 = f32[4096]{0:T(1024)S(1)} all-reduce(f32[4096]{0:T(1024)S(1)} %multiply_reduce_fusion.5), channel_id=1, replica_groups=mesh['batch'=4,'row'=4,'col'=2] {'row'}, use_global_device_ids=true, to_apply=%region_4.0 | all-reduce | flops 4096 | bytes 32768 | tf_op jit(solution)/shard_map/while/body/eval_jaxpr/psum | solution.py:21
  96.4 1.5 dynamic_update_slice.19
  97.9 1.4 dynamic_update_slice.18
  99.3 12.2 %multiply_reduce_fusion.4 = f32[2048]{0:T(1024)S(1)} fusion(f32[2048,4096]{1,0:T(8,128)} %get-tuple-element.232, f32[4096]{0:T(1024)S(1)} %broadcast_select_fusion.2), kind=kLoop, calls=%fused_computation.1.clone.1 | loop fusion | flops 16775168 | bytes 33579008 | tf_op jit(solution)/shard_map/while/body/eval_jaxpr/reduce_sum | solution.py:17
  111.6 5.0 %psum.26 = f32[2048]{0:T(1024)S(1)} all-reduce(f32[2048]{0:T(1024)S(1)} %multiply_reduce_fusion.4), channel_id=1, replica_groups=mesh['batch'=4,'row'=4,'col'=2] {'col'}, use_global_device_ids=true, to_apply=%region_2.0 | all-reduce | flops 2048 | bytes 16384 | tf_op jit(solution)/shard_map/while/body/eval_jaxpr/psum | solution.py:18
  116.6 12.8 %multiply_reduce_fusion.5 = f32[4096]{0:T(1024)S(1)} fusion(f32[2048,4096]{1,0:T(8,128)} %get-tuple-element.232, f32[2048]{0:T(1024)S(1)} %div.18), kind=kLoop, calls=%fused_computation.clone.1 | loop fusion | flops 16773120 | bytes 33579008 | tf_op jit(solution)/shard_map/while/body/eval_jaxpr/reduce_sum | solution.py:20
  129.4 10.1 %psum.27 = f32[4096]{0:T(1024)S(1)} all-reduce(f32[4096]{0:T(1024)S(1)} %multiply_reduce_fusion.5), channel_id=1, replica_groups=mesh['batch'=4,'row'=4,'col'=2] {'row'}, use_global_device_ids=true, to_apply=%region_4.0 | all-reduce | flops 4096 | bytes 32768 | tf_op jit(solution)/shard_map/while/body/eval_jaxpr/psum | solution.py:21
  139.5 1.5 dynamic_update_slice.19
  141.1 1.4 dynamic_update_slice.18
  142.5 12.2 %multiply_reduce_fusion.4 = f32[2048]{0:T(1024)S(1)} fusion(f32[2048,4096]{1,0:T(8,128)} %get-tuple-element.232, f32[4096]{0:T(1024)S(1)} %broadcast_select_fusion.2), kind=kLoop, calls=%fused_computation.1.clone.1 | loop fusion | flops 16775168 | bytes 33579008 | tf_op jit(solution)/shard_map/while/body/eval_jaxpr/reduce_sum | solution.py:17
  154.7 5.0 %psum.26 = f32[2048]{0:T(1024)S(1)} all-reduce(f32[2048]{0:T(1024)S(1)} %multiply_reduce_fusion.4), channel_id=1, replica_groups=mesh['batch'=4,'row'=4,'col'=2] {'col'}, use_global_device_ids=true, to_apply=%region_2.0 | all-reduce | flops 2048 | bytes 16384 | tf_op jit(solution)/shard_map/while/body/eval_jaxpr/psum | solution.py:18
  159.7 12.8 %multiply_reduce_fusion.5 = f32[4096]{0:T(1024)S(1)} fusion(f32[2048,4096]{1,0:T(8,128)} %get-tuple-element.232, f32[2048]{0:T(1024)S(1)} %div.18), kind=kLoop, calls=%fused_computation.clone.1 | loop fusion | flops 16773120 | bytes 33579008 | tf_op jit(solution)/shard_map/while/body/eval_jaxpr/reduce_sum | solution.py:20
  172.5 10.1 %psum.27 = f32[4096]{0:T(1024)S(1)} all-reduce(f32[4096]{0:T(1024)S(1)} %multiply_reduce_fusion.5), channel_id=1, replica_groups=mesh['batch'=4,'row'=4,'col'=2] {'row'}, use_global_device_ids=true, to_apply=%region_4.0 | all-reduce | flops 4096 | bytes 32768 | tf_op jit(solution)/shard_map/while/body/eval_jaxpr/psum | solution.py:21
  182.7 1.5 dynamic_update_slice.19
  184.2 1.4 dynamic_update_slice.18
  (16 shorter events, 0.1 us)
Async XLA Ops:
  12.6 42.4 %copy-start = (s32[4096]{0:T(1024)S(1)}, s32[4096]{0:T(1024)}, u32[]{:S(2)}) copy-start(s32[4096]{0:T(1024)} %param.9) | copy-start | bytes 49156
  12.6 42.5 %copy-start.1 = (s32[2048]{0:T(1024)S(1)}, s32[2048]{0:T(1024)}, u32[]{:S(2)}) copy-start(s32[2048]{0:T(1024)} %param.8) | copy-start | bytes 24580
where the time goes:
time: 187 us; the launch traced here: 186 us
  other arithmetic  118 us (63%)
  blocking collectives  46.5 us (25%)
  local copies, waits for them, and re-layouts  20.1 us (11%)
    mul x1, other arithmetic, shards(): flows.reshape(row_count // tile_side, tile_side, col_count // tile_side,...  42.4 us
    reduce_sum x3, other arithmetic, advance(): col_part = jnp.sum(active * row_scale[:, None], axis=0)  38.4 us
    reduce_sum x3, other arithmetic, advance(): row_part = jnp.sum(active * col_scale[None, :], axis=1)  36.8 us
    psum x3, blocking collectives, advance(): col_total = lax.psum(col_part, 'row')  30.5 us
    psum x3, blocking collectives, advance(): row_total = lax.psum(row_part, 'col')  16 us
    mul x1, local copies, waits for them, and re-layouts, shards(): flows.reshape(row_count // tile_side, tile_side, col_count // tile_side,...  11.2 us
    dynamic_update_slice x3, local copies, waits for them, and re-layouts, advance(): lax.dynamic_update_slice_in_dim(col_hist, col_scale[None, :], sweep_index...  4.64 us
    dynamic_update_slice x3, local copies, waits for them, and re-layouts, advance(): lax.dynamic_update_slice_in_dim(row_hist, row_scale[None, :], sweep_index...  4.23 us

commit v1 on v0

--- a/solution.py
+++ b/solution.py
@@ -18,7 +18,7 @@
         row_total = lax.psum(row_part, "col")
         row_scale = row_goal / row_total
         col_part = jnp.sum(active * row_scale[:, None], axis=0)
-        col_total = lax.psum(col_part, "row")
+        col_total = jnp.sum(lax.all_gather(col_part, "row"), axis=0)
         col_scale = col_goal / col_total
         row_hist = lax.dynamic_update_slice_in_dim(row_hist, row_scale[None, :], sweep_index, 0)
         col_hist = lax.dynamic_update_slice_in_dim(col_hist, col_scale[None, :], sweep_index, 0)

time: 187 us -> 172 us (0.920)
  blocking collectives: 46.5 us -> 31.7 us
    psum x3 -> x0, blocking collectives: 30.5 us -> none  [advance(): col_total = lax.psum(col_part, 'row')]
    all_gather x0 -> x3, blocking collectives: none -> 15.7 us  [advance(): col_total = jnp.sum(lax.all_gather(col_part, 'row'), axis=0)]
where the time goes in v1:
time: 172 us; the launch traced here: 171 us
  other arithmetic  118 us (69%)
  blocking collectives  31.7 us (18%)
  local copies, waits for them, and re-layouts  20.2 us (12%)
    mul x1, other arithmetic, shards(): flows.reshape(row_count // tile_side, tile_side, col_count // tile_side,...  42.4 us
    reduce_sum x3, other arithmetic, advance(): col_part = jnp.sum(active * row_scale[:, None], axis=0)  38.3 us
    reduce_sum x3, other arithmetic, advance(): row_part = jnp.sum(active * col_scale[None, :], axis=1)  36.8 us
    psum x3, blocking collectives, advance(): row_total = lax.psum(row_part, 'col')  16 us
    all_gather x3, blocking collectives, advance(): col_total = jnp.sum(lax.all_gather(col_part, 'row'), axis=0)  15.7 us
    mul x1, local copies, waits for them, and re-layouts, shards(): flows.reshape(row_count // tile_side, tile_side, col_count // tile_side,...  11.2 us
    dynamic_update_slice x3, local copies, waits for them, and re-layouts, advance(): lax.dynamic_update_slice_in_dim(col_hist, col_scale[None, :], sweep_index...  4.65 us
    dynamic_update_slice x3, local copies, waits for them, and re-layouts, advance(): lax.dynamic_update_slice_in_dim(row_hist, row_scale[None, :], sweep_index...  4.23 us

profile of v1, /device:TPU:0, one launch (start us, length us, event | category | flops | bytes accessed | tf_op | source)
XLA Modules:
  0.0 171.1 jit_solution(4734910486168793281)
XLA Ops:
  0.6 0.7 convert_element_type.9
  1.3 11.2 %mul.63 = f32[16,128,32,128]{3,2,1,0:T(8,128)} broadcast(f32[16,32]{1,0:T(8,128)S(1)} %convert_element_type.9), dimensions={0,2} | broadcast | bytes 33556480 | tf_op jit(solution)/shard_map/mul | solution.py:38
  12.6 42.4 %bitcast_multiply_fusion = f32[2048,4096]{1,0:T(8,128)} fusion(f32[2048,4096]{1,0:T(8,128)} %param.6, f32[256,8,32,128]{3,2,1,0:T(8,128)} %bitcast.10), kind=kLoop, calls=%fused_computation.3 | loop fusion | flops 8388608 | bytes 100663296 | tf_op jit(solution)/shard_map/mul | solution.py:38
  55.0 0.0 copy-done
  55.0 0.0 copy-done.1
  55.0 116.1 %while.18 = (s32[]{:T(128)}, f32[4096]{0:T(1024)S(1)}, f32[3,2048]{1,0:T(4,128)}, f32[3,4096]{1,0:T(4,128)}, f32[2048,4096]{1,0:T(8,128)}, /*index=5*/f32[2048]{...) while((s32[]{:T(128)}, f32[4096]{0:T(1024)S(1)}, f32[3,2048]{1,0:T(4,128)}, ...), condition=%wide.region_5.0_spmd.clone, body=%wide.region_0.0_spmd.clone.sunk | while | flops 33572864 | bytes 67625080 | solution.py:27
  55.1 12.3 %multiply_reduce_fusion.4 = f32[2048]{0:T(1024)S(1)} fusion(f32[2048,4096]{1,0:T(8,128)} %get-tuple-element.234, f32[4096]{0:T(1024)S(1)} %broadcast_select_fusion.2), kind=kLoop, calls=%fused_computation.1.clone.1 | loop fusion | flops 16775168 | bytes 33579008 | tf_op jit(solution)/shard_map/while/body/eval_jaxpr/reduce_sum | solution.py:17
  67.3 6.0 %psum.13 = f32[2048]{0:T(1024)S(1)} all-reduce(f32[2048]{0:T(1024)S(1)} %multiply_reduce_fusion.4), channel_id=1, replica_groups=mesh['batch'=4,'row'=4,'col'=2] {'col'}, use_global_device_ids=true, to_apply=%region_2.0 | all-reduce | flops 2048 | bytes 16384 | tf_op jit(solution)/shard_map/while/body/eval_jaxpr/psum | solution.py:18
  73.3 12.8 %multiply_reduce_fusion.5 = f32[4096]{0:T(1024)S(1)} fusion(f32[2048,4096]{1,0:T(8,128)} %get-tuple-element.234, f32[2048]{0:T(1024)S(1)} %div.31), kind=kLoop, calls=%fused_computation.clone.1 | loop fusion | flops 16773120 | bytes 33579008 | tf_op jit(solution)/shard_map/while/body/eval_jaxpr/reduce_sum | solution.py:20
  86.1 5.2 %all-gather.3 = f32[16384]{0:T(1024)S(1)} all-gather(f32[4096]{0:T(1024)S(1)} %multiply_reduce_fusion.5), channel_id=2, replica_groups=mesh['batch'=4,'row'=4,'col'=2] {'row'}, dimensions={0}, use_global_device_ids=true | all-gather | bytes 81920 | tf_op jit(solution)/shard_map/while/body/eval_jaxpr/all_gather | solution.py:21
  91.4 1.5 dynamic_update_slice.19
  93.0 1.4 dynamic_update_slice.18
  94.4 12.2 %multiply_reduce_fusion.4 = f32[2048]{0:T(1024)S(1)} fusion(f32[2048,4096]{1,0:T(8,128)} %get-tuple-element.234, f32[4096]{0:T(1024)S(1)} %broadcast_select_fusion.2), kind=kLoop, calls=%fused_computation.1.clone.1 | loop fusion | flops 16775168 | bytes 33579008 | tf_op jit(solution)/shard_map/while/body/eval_jaxpr/reduce_sum | solution.py:17
  106.6 5.0 %psum.13 = f32[2048]{0:T(1024)S(1)} all-reduce(f32[2048]{0:T(1024)S(1)} %multiply_reduce_fusion.4), channel_id=1, replica_groups=mesh['batch'=4,'row'=4,'col'=2] {'col'}, use_global_device_ids=true, to_apply=%region_2.0 | all-reduce | flops 2048 | bytes 16384 | tf_op jit(solution)/shard_map/while/body/eval_jaxpr/psum | solution.py:18
  111.7 12.8 %multiply_reduce_fusion.5 = f32[4096]{0:T(1024)S(1)} fusion(f32[2048,4096]{1,0:T(8,128)} %get-tuple-element.234, f32[2048]{0:T(1024)S(1)} %div.31), kind=kLoop, calls=%fused_computation.clone.1 | loop fusion | flops 16773120 | bytes 33579008 | tf_op jit(solution)/shard_map/while/body/eval_jaxpr/reduce_sum | solution.py:20
  124.4 5.2 %all-gather.3 = f32[16384]{0:T(1024)S(1)} all-gather(f32[4096]{0:T(1024)S(1)} %multiply_reduce_fusion.5), channel_id=2, replica_groups=mesh['batch'=4,'row'=4,'col'=2] {'row'}, dimensions={0}, use_global_device_ids=true | all-gather | bytes 81920 | tf_op jit(solution)/shard_map/while/body/eval_jaxpr/all_gather | solution.py:21
  129.8 1.5 dynamic_update_slice.19
  131.3 1.4 dynamic_update_slice.18
  132.7 12.2 %multiply_reduce_fusion.4 = f32[2048]{0:T(1024)S(1)} fusion(f32[2048,4096]{1,0:T(8,128)} %get-tuple-element.234, f32[4096]{0:T(1024)S(1)} %broadcast_select_fusion.2), kind=kLoop, calls=%fused_computation.1.clone.1 | loop fusion | flops 16775168 | bytes 33579008 | tf_op jit(solution)/shard_map/while/body/eval_jaxpr/reduce_sum | solution.py:17
  145.0 5.0 %psum.13 = f32[2048]{0:T(1024)S(1)} all-reduce(f32[2048]{0:T(1024)S(1)} %multiply_reduce_fusion.4), channel_id=1, replica_groups=mesh['batch'=4,'row'=4,'col'=2] {'col'}, use_global_device_ids=true, to_apply=%region_2.0 | all-reduce | flops 2048 | bytes 16384 | tf_op jit(solution)/shard_map/while/body/eval_jaxpr/psum | solution.py:18
  150.0 12.8 %multiply_reduce_fusion.5 = f32[4096]{0:T(1024)S(1)} fusion(f32[2048,4096]{1,0:T(8,128)} %get-tuple-element.234, f32[2048]{0:T(1024)S(1)} %div.31), kind=kLoop, calls=%fused_computation.clone.1 | loop fusion | flops 16773120 | bytes 33579008 | tf_op jit(solution)/shard_map/while/body/eval_jaxpr/reduce_sum | solution.py:20
  162.8 5.2 %all-gather.3 = f32[16384]{0:T(1024)S(1)} all-gather(f32[4096]{0:T(1024)S(1)} %multiply_reduce_fusion.5), channel_id=2, replica_groups=mesh['batch'=4,'row'=4,'col'=2] {'row'}, dimensions={0}, use_global_device_ids=true | all-gather | bytes 81920 | tf_op jit(solution)/shard_map/while/body/eval_jaxpr/all_gather | solution.py:21
  168.1 1.5 dynamic_update_slice.19
  169.7 1.4 dynamic_update_slice.18
  (22 shorter events, 0.3 us)
Async XLA Ops:
  12.6 42.4 %copy-start = (s32[4096]{0:T(1024)S(1)}, s32[4096]{0:T(1024)}, u32[]{:S(2)}) copy-start(s32[4096]{0:T(1024)} %param.9) | copy-start | bytes 49156
  12.6 42.5 %copy-start.1 = (s32[2048]{0:T(1024)S(1)}, s32[2048]{0:T(1024)}, u32[]{:S(2)}) copy-start(s32[2048]{0:T(1024)} %param.8) | copy-start | bytes 24580
